TPU v7x, 32 devices: a whole 2x2x4 slice. The times are simulated.
32 devices in a mesh: shift: 16 (over z, x, core), row: 2 (over y).
Axes of the slice: x: 2, y: 2, z: 4, core: 2. Of those that a mesh axis runs over, the one named last changes fastest.
Arguments:
- solutions: bfloat16 [32, 2, 2048, 128], P('shift', None, 'row'), may hold values from -96 to 96
Outputs:
- moments: bfloat16 [2, 8, 2048, 128], P(None, None, ('row', 'shift'))
- gram_real: float32 [1024, 1024], replicated
- gram_imag: float32 [1024, 1024], replicated
All inputs are finite; a program needn't handle non-finite values.
Results may differ from a plain program's by a relative error of at most 0.0061.
Values may be sent and summed in bfloat16 or wider, within the bound.
A program may use at most 64 MiB of HBM per device.

v0:
```python
import math
import jax
import jax.numpy as jnp
from jax import lax
from jax.sharding import PartitionSpec as P

PANELS = 8


def coefficient_block(first_shift, shift_count, all_shifts, panels):
    indices = (first_shift + jnp.arange(shift_count, dtype=jnp.int32)).astype(jnp.float32)
    orders = jnp.arange(1, panels + 1, dtype=jnp.int32).astype(jnp.float32)
    angles = orders[:, None] * (2.0 * math.pi * (indices + 0.5) / all_shifts)[None, :]
    cos_part = jnp.cos(angles) / all_shifts
    sin_part = jnp.sin(angles) / all_shifts
    real_row = jnp.stack([cos_part, -sin_part], axis=-1)
    imag_row = jnp.stack([sin_part, cos_part], axis=-1)
    return (
        jnp.stack([real_row, imag_row], axis=0)
        .reshape(2 * panels, 2 * shift_count)
        .astype(jnp.bfloat16)
    )


def weigh(block_data, first_shift, all_shifts):
    shift_count = block_data.shape[0]
    weights = coefficient_block(first_shift, shift_count, all_shifts, PANELS)
    flat = block_data.reshape(2 * shift_count, -1)
    product = jnp.dot(weights, flat, preferred_element_type=jnp.float32)
    return product.reshape(2, PANELS, block_data.shape[2], block_data.shape[3])


def pair_product(left, right):
    width = left.shape[0] * left.shape[2]
    return jnp.einsum("krl,qrm->klqm", left, right, preferred_element_type=jnp.float32).reshape(
        width, width
    )


def gram_terms(moment_block):
    real_part = moment_block[0]
    imag_part = moment_block[1]
    gram_real = pair_product(real_part, real_part) + pair_product(imag_part, imag_part)
    gram_imag = pair_product(real_part, imag_part) - pair_product(imag_part, real_part)
    return (gram_real, gram_imag)


def local(solutions):
    shift_count = solutions.shape[0]
    all_shifts = shift_count * lax.axis_size("shift")
    moment_sum = weigh(
        lax.all_to_all(solutions, "shift", split_axis=2, concat_axis=0, tiled=True), 0, all_shifts
    )
    moments = moment_sum.astype(jnp.bfloat16)
    row_count = moments.shape[2] * lax.axis_size("shift") * lax.axis_size("row")
    shard_real, shard_imag = gram_terms(moments)
    gram_real, gram_imag = lax.psum((shard_real, shard_imag), ("shift", "row"))
    factor = 1.0 / math.sqrt(row_count)
    return (moments, gram_real * factor, gram_imag * factor)


def solution(mesh):
    placed = (P("shift", None, "row", None),)
    return jax.shard_map(
        local,
        mesh=mesh,
        in_specs=placed,
        out_specs=(P(None, None, ("row", "shift"), None), P(), P()),
        check_vma=False,
    )
```

profile of v0, /device:TPU:0, one launch (start us, length us, event | category | flops | bytes accessed | tf_op | source)
XLA Modules:
  0.0 245.7 jit_solution(16448146008260359767)
XLA Ops:
  7.2 3.3 %copy.14 = bf16[2,2,1024,128]{3,1,0,2:T(2,128)(2,1)} copy(bf16[2,2,1024,128]{3,2,1,0:T(8,128)(2,1)} %param.1) | data formatting | bytes 2097152 | tf_op args[0]
  10.4 7.4 %all-to-all-start = ((bf16[2,2,1024,128]{3,1,0,2:T(2,128)(2,1)}), bf16[2,2,1024,128]{3,1,0,2:T(2,128)(2,1)S(1)}, u32[]{:S(2)}, u32[]{:S(2)}) async-start(bf16[2,2,1024,128]{3,1,0,2:T(2,128)(2,1)} %copy.14), calls=%async_computation | async-start | bytes 2097152 | tf_op jit(solution)/shard_map/all_to_all | solution.py:52
  17.8 0.0 all-reduce.3.cloned.1.call-start
  17.9 0.1 fusion.20
  18.0 0.1 copy.10
  18.1 0.1 copy.12
  18.2 0.1 copy.11
  18.3 0.1 copy.13
  18.4 22.3 %all-to-all-done = bf16[2,2,1024,128]{3,1,0,2:T(2,128)(2,1)S(1)} async-done(((bf16[2,2,1024,128]{3,1,0,2:T(2,128)(2,1)}), bf16[2,2,1024,128]{3,1,0,2:T(2,128)(2,1)S(1)}, u32[]{:S(2)}, u32[]{:S(2)}) %all-to-all-start) | async-done | bytes 1048608 | tf_op jit(solution)/shard_map/all_to_all | solution.py:52
  40.7 0.3 copy.15
  41.0 0.7 convolution_convert_fusion
  41.7 0.7 fusion.7
  42.4 0.7 fusion.2
  43.2 2.8 %convolution_subtract_fusion = f32[1024,1024]{1,0:T(8,128)} fusion(f32[1024,1024]{1,0:T(8,128)S(1)} %fusion.2, bf16[8,8,8,128]{3,2,1,0:T(8,128)(2,1)S(1)} %bitcast.54, bf16[8,8,8,128]{3,2,1,0:T(8,128)(2,1)S(1)} %bitcast.58), kind=kOutput, calls=%fused_computation | convolution fusion | flops 135266304 | bytes 8650752 | tf_op jit(solution)/shard_map/krl,qrm->klqm/dot_general | solution.py:35
  45.9 2.7 %convolution_add_fusion = f32[1024,1024]{1,0:T(8,128)} fusion(f32[1024,1024]{1,0:T(8,128)S(1)} %fusion.7, bf16[8,8,8,128]{3,2,1,0:T(8,128)(2,1)S(1)} %bitcast.55), kind=kOutput, calls=%fused_computation.1 | convolution fusion | flops 135266304 | bytes 8519680 | tf_op jit(solution)/shard_map/krl,qrm->klqm/dot_general | solution.py:35
  48.6 0.0 all-reduce.3.cloned.1.call-update
  48.7 0.8 copy.17
  49.4 180.6 %all-reduce.3.cloned.1.call-done = (f32[1024,1024]{1,0:T(8,128)}, f32[1024,1024]{1,0:T(8,128)}) async-done(((f32[1024,1024]{1,0:T(8,128)}, f32[1024,1024]{1,0:T(8,128)}), (f32[1024,1024]{1,0:T(8,128)}, f32[1024,1024]{1,0:T(8,128)})) %all-reduce.3.cloned.1.call-update) | async-done | bytes 8388624 | tf_op jit(solution)/shard_map/psum | solution.py:57
  230.0 8.9 %broadcast_multiply_fusion = (f32[1024,1024]{1,0:T(8,128)}, f32[1024,1024]{1,0:T(8,128)}) fusion(f32[1024,1024]{1,0:T(8,128)} %get-tuple-element.13, f32[1024,1024]{1,0:T(8,128)} %get-tuple-element.12), kind=kLoop, calls=%fused_computation.2 | loop fusion | flops 2097152 | bytes 16777216 | tf_op jit(solution)/shard_map/mul | solution.py:59
  (4 shorter events, 0.0 us)
Async XLA Ops:
  10.4 30.3 %all-to-all-start = ((bf16[2,2,1024,128]{3,1,0,2:T(2,128)(2,1)}), bf16[2,2,1024,128]{3,1,0,2:T(2,128)(2,1)S(1)}, u32[]{:S(2)}, u32[]{:S(2)}) async-start(bf16[2,2,1024,128]{3,1,0,2:T(2,128)(2,1)} %copy.14), calls=%async_computation | async-start | bytes 2097152 | tf_op jit(solution)/shard_map/all_to_all | solution.py:52
  17.8 212.2 %all-reduce.3.cloned.1.call-start = ((), (), s32[]{:S(2)}) async-start(), calls=%async_computation.1 | async-start | bytes 16777216 | tf_op jit(solution)/shard_map/psum | solution.py:57
Sparse Core Ops, SparseCore 0:
  48.8 181.2 all-reduce.2
where the time goes:
time: 246 us
  waiting for transfers between devices  203 us (83%)
  between operations  14.1 us (6%)
  other arithmetic  8.99 us (4%)
  matrix products  7.62 us (3%)
  starting transfers between devices  7.43 us (3%)
  local copies, waits for them, and re-layouts  4.65 us (2%)
    psum x1, waiting for transfers between devices, local(): gram_real, gram_imag = lax.psum((shard_real, shard_imag), ('shift', 'row'))  181 us
    all_to_all x1, waiting for transfers between devices, local(): lax.all_to_all(solutions, 'shift', split_axis=2, concat_axis=0, tiled=True)  22.3 us
    mul x1, other arithmetic, local(): return (moments, gram_real * factor, gram_imag * factor)  8.85 us
    all_to_all x1, starting transfers between devices, local(): lax.all_to_all(solutions, 'shift', split_axis=2, concat_axis=0, tiled=True)  7.39 us
    dot_general x4, matrix products, pair_product(): jnp.einsum('krl,qrm->klqm', left, right, preferred_element_type=jnp.float32)  6.95 us
  transfers between devices with their start and end apart: 2, of which 2 were waited for; matrix products, arithmetic and copies ran while one was open for 0% of the time, Pallas kernels for 0%

commit v1 on v0

--- a/solution.py
+++ b/solution.py
@@ -49,7 +49,14 @@
     shift_count = solutions.shape[0]
     all_shifts = shift_count * lax.axis_size("shift")
     moment_sum = weigh(
-        lax.all_to_all(solutions, "shift", split_axis=2, concat_axis=0, tiled=True), 0, all_shifts
+        jnp.concatenate(
+            lax.all_to_all(
+                jnp.stack(jnp.split(solutions, lax.axis_size("shift"), axis=2)), "shift", 0, 0
+            ),
+            axis=0,
+        ),
+        0,
+        all_shifts,
     )
     moments = moment_sum.astype(jnp.bfloat16)
     row_count = moments.shape[2] * lax.axis_size("shift") * lax.axis_size("row")

time: 246 us -> 267 us (1.085)
  local copies, waits for them, and re-layouts: 4.65 us -> 24.7 us
    unnamed x2 -> x16, local copies, waits for them, and re-layouts: 4.03 us -> 22.9 us
where the time goes in v1:
time: 267 us; the launch traced here: 266 us
  waiting for transfers between devices  203 us (76%)
  local copies, waits for them, and re-layouts  24.7 us (9%)
  between operations  14.1 us (5%)
  other arithmetic  8.99 us (3%)
  matrix products  7.61 us (3%)
  starting transfers between devices  7.43 us (3%)
    psum x1, waiting for transfers between devices, local(): gram_real, gram_imag = lax.psum((shard_real, shard_imag), ('shift', 'row'))  181 us
    unnamed x16, local copies, waits for them, and re-layouts  22.9 us
    all_to_all x1, waiting for transfers between devices, local(): lax.all_to_all(jnp.stack(jnp.split(solutions, lax.axis_size('shift'), axi...  22.3 us
    mul x1, other arithmetic, local(): return (moments, gram_real * factor, gram_imag * factor)  8.85 us
    all_to_all x1, starting transfers between devices, local(): lax.all_to_all(jnp.stack(jnp.split(solutions, lax.axis_size('shift'), axi...  7.39 us
    dot_general x4, matrix products, pair_product(): jnp.einsum('krl,qrm->klqm', left, right, preferred_element_type=jnp.float32)  6.95 us
  transfers between devices with their start and end apart: 2, of which 2 were waited for; matrix products, arithmetic and copies ran while one was open for 0% of the time, Pallas kernels for 0%

profile of v1, /device:TPU:0, one launch (start us, length us, event | category | flops | bytes accessed | tf_op | source)
XLA Modules:
  0.0 265.8 jit_solution(7049309099060135210)
XLA Ops:
  7.2 1.5 bitcast_dynamic-update-slice_fusion.15
  8.6 1.5 bitcast_dynamic-update-slice_fusion.14
  10.1 1.5 bitcast_dynamic-update-slice_fusion.13
  11.6 1.5 bitcast_dynamic-update-slice_fusion.12
  13.1 1.5 bitcast_dynamic-update-slice_fusion.11
  14.5 1.5 bitcast_dynamic-update-slice_fusion.10
  16.0 1.5 bitcast_dynamic-update-slice_fusion.9
  17.5 1.5 bitcast_dynamic-update-slice_fusion.8
  19.0 1.5 bitcast_dynamic-update-slice_fusion.7
  20.4 1.5 bitcast_dynamic-update-slice_fusion.6
  21.9 1.5 bitcast_dynamic-update-slice_fusion.5
  23.4 1.5 bitcast_dynamic-update-slice_fusion.4
  24.9 1.5 bitcast_dynamic-update-slice_fusion.3
  26.3 1.5 bitcast_dynamic-update-slice_fusion.2
  27.8 1.5 bitcast_dynamic-update-slice_fusion.1
  29.3 1.5 bitcast_dynamic-update-slice_fusion
  30.7 7.4 %all-to-all-start = ((bf16[16,2,2,64,128]{4,3,2,1,0:T(8,128)(2,1)}), bf16[16,2,2,64,128]{4,3,2,1,0:T(8,128)(2,1)S(1)}, u32[]{:S(2)}, u32[]{:S(2)}) async-start(bf16[16,2,2,64,128]{4,3,2,1,0:T(8,128)(2,1)} %bitcast_dynamic-update-slice_fusion), calls=%async_computation | async-start | bytes 2097152 | tf_op jit(solution)/shard_map/all_to_all | solution.py:53
  38.7 22.3 %all-to-all-done = bf16[16,2,2,64,128]{4,3,2,1,0:T(8,128)(2,1)S(1)} async-done(((bf16[16,2,2,64,128]{4,3,2,1,0:T(8,128)(2,1)}), bf16[16,2,2,64,128]{4,3,2,1,0:T(8,128)(2,1)S(1)}, u32[]{:S(2)}, u32[]{:S(2)}) %all-to-all-start) | async-done | bytes 1048608 | tf_op jit(solution)/shard_map/all_to_all | solution.py:53
  62.4 0.7 fusion.2
  63.2 2.7 %convolution_subtract_fusion = f32[1024,1024]{1,0:T(8,128)} fusion(f32[1024,1024]{1,0:T(8,128)S(1)} %fusion.2, bf16[8,8,8,128]{3,2,1,0:T(8,128)(2,1)S(1)} %bitcast.83, bf16[8,8,8,128]{3,2,1,0:T(8,128)(2,1)S(1)} %bitcast.87), kind=kOutput, calls=%fused_computation | convolution fusion | flops 135266304 | bytes 8650752 | tf_op jit(solution)/shard_map/krl,qrm->klqm/dot_general | solution.py:35
  65.9 2.7 %convolution_add_fusion = f32[1024,1024]{1,0:T(8,128)} fusion(f32[1024,1024]{1,0:T(8,128)S(1)} %fusion.7, bf16[8,8,8,128]{3,2,1,0:T(8,128)(2,1)S(1)} %bitcast.84), kind=kOutput, calls=%fused_computation.1 | convolution fusion | flops 135266304 | bytes 8519680 | tf_op jit(solution)/shard_map/krl,qrm->klqm/dot_general | solution.py:35
  68.7 0.8 copy.14
  69.5 180.6 %all-reduce.3.cloned.1.call-done = (f32[1024,1024]{1,0:T(8,128)}, f32[1024,1024]{1,0:T(8,128)}) async-done(((f32[1024,1024]{1,0:T(8,128)}, f32[1024,1024]{1,0:T(8,128)}), (f32[1024,1024]{1,0:T(8,128)}, f32[1024,1024]{1,0:T(8,128)})) %all-reduce.3.cloned.1.call-update) | async-done | bytes 8388624 | tf_op jit(solution)/shard_map/psum | solution.py:64
  250.1 8.9 %broadcast_multiply_fusion = (f32[1024,1024]{1,0:T(8,128)}, f32[1024,1024]{1,0:T(8,128)}) fusion(f32[1024,1024]{1,0:T(8,128)} %get-tuple-element.13, f32[1024,1024]{1,0:T(8,128)} %get-tuple-element.12), kind=kLoop, calls=%fused_computation.2 | loop fusion | flops 2097152 | bytes 16777216 | tf_op jit(solution)/shard_map/mul | solution.py:66
  (13 shorter events, 1.9 us)
Async XLA Ops:
  30.7 30.3 %all-to-all-start = ((bf16[16,2,2,64,128]{4,3,2,1,0:T(8,128)(2,1)}), bf16[16,2,2,64,128]{4,3,2,1,0:T(8,128)(2,1)S(1)}, u32[]{:S(2)}, u32[]{:S(2)}) async-start(bf16[16,2,2,64,128]{4,3,2,1,0:T(8,128)(2,1)} %bitcast_dynamic-update-slice_fusion), calls=%async_computation | async-start | bytes 2097152 | tf_op jit(solution)/shard_map/all_to_all | solution.py:53
  38.1 211.9 %all-reduce.3.cloned.1.call-start = ((), (), s32[]{:S(2)}) async-start(), calls=%async_computation.1 | async-start | bytes 16777216 | tf_op jit(solution)/shard_map/psum | solution.py:64
Sparse Core Ops, SparseCore 0:
  68.8 181.2 all-reduce.2

commit v2 on v0

--- a/solution.py
+++ b/solution.py
@@ -54,7 +54,7 @@
     moments = moment_sum.astype(jnp.bfloat16)
     row_count = moments.shape[2] * lax.axis_size("shift") * lax.axis_size("row")
     shard_real, shard_imag = gram_terms(moments)
-    gram_real, gram_imag = lax.psum((shard_real, shard_imag), ("shift", "row"))
+    gram_real, gram_imag = lax.psum(lax.psum((shard_real, shard_imag), "row"), "shift")
     factor = 1.0 / math.sqrt(row_count)
     return (moments, gram_real * factor, gram_imag * factor)
 

time: 246 us -> 439 us (1.78)
  waiting for transfers between devices: 203 us -> 396 us
    psum x1 -> x2, waiting for transfers between devices: 181 us -> 374 us  [the longest x1 200 us: local(): lax.psum((shard_real, shard_imag), 'row')]
  transfers between devices with their start and end apart: 2 -> 3, of which waited for: 2 -> 3; matrix products, arithmetic and copies ran while one was open for 0% -> 0% of each run, Pallas kernels for 0% -> 0%
where the time goes in v2:
time: 439 us
  waiting for transfers between devices  396 us (90%)
  between operations  14.1 us (3%)
  other arithmetic  8.99 us (2%)
  matrix products  7.62 us (2%)
  starting transfers between devices  7.47 us (2%)
  local copies, waits for them, and re-layouts  4.65 us (1%)
    psum x1, waiting for transfers between devices, local(): lax.psum((shard_real, shard_imag), 'row')  200 us
    psum x1, waiting for transfers between devices, local(): lax.psum(lax.psum((shard_real, shard_imag), 'row'), 'shift')  173 us
    all_to_all x1, waiting for transfers between devices, local(): lax.all_to_all(solutions, 'shift', split_axis=2, concat_axis=0, tiled=True)  22.3 us
    mul x1, other arithmetic, local(): return (moments, gram_real * factor, gram_imag * factor)  8.85 us
  transfers between devices with their start and end apart: 3, of which 3 were waited for; matrix products, arithmetic and copies ran while one was open for 0% of the time, Pallas kernels for 0%

profile of v2, /device:TPU:0, one launch (start us, length us, event | category | flops | bytes accessed | tf_op | source)
XLA Modules:
  0.0 439.0 jit_solution(12760115862139067368)
XLA Ops:
  7.2 3.3 copy.14
  10.4 7.4 %all-to-all-start = ((bf16[2,2,1024,128]{3,1,0,2:T(2,128)(2,1)}), bf16[2,2,1024,128]{3,1,0,2:T(2,128)(2,1)S(1)}, u32[]{:S(2)}, u32[]{:S(2)}) async-start(bf16[2,2,1024,128]{3,1,0,2:T(2,128)(2,1)} %copy.14), calls=%async_computation | async-start | bytes 2097152 | tf_op jit(solution)/shard_map/all_to_all | solution.py:52
  17.8 0.0 all-reduce.7.cloned.1.call-start
  17.9 0.1 fusion.20
  18.0 0.1 copy.10
  18.1 0.1 copy.12
  18.2 0.1 copy.11
  18.3 0.1 copy.13
  18.4 22.3 %all-to-all-done = bf16[2,2,1024,128]{3,1,0,2:T(2,128)(2,1)S(1)} async-done(((bf16[2,2,1024,128]{3,1,0,2:T(2,128)(2,1)}), bf16[2,2,1024,128]{3,1,0,2:T(2,128)(2,1)S(1)}, u32[]{:S(2)}, u32[]{:S(2)}) %all-to-all-start) | async-done | bytes 1048608 | tf_op jit(solution)/shard_map/all_to_all | solution.py:52
  40.7 0.3 copy.15
  41.0 0.7 convolution_convert_fusion
  41.7 0.7 fusion.7
  42.4 0.7 fusion.2
  43.2 2.8 convolution_subtract_fusion
  45.9 2.7 convolution_add_fusion
  48.6 0.0 all-reduce.7.cloned.1.call-update
  48.7 0.0 all-reduce.5.cloned.1.call-start
  48.7 200.3 %all-reduce.7.cloned.1.call-done = (f32[1024,1024]{1,0:T(8,128)}, f32[1024,1024]{1,0:T(8,128)}) async-done(((f32[1024,1024]{1,0:T(8,128)}, f32[1024,1024]{1,0:T(8,128)}), (f32[1024,1024]{1,0:T(8,128)}, f32[1024,1024]{1,0:T(8,128)})) %all-reduce.7.cloned.1.call-update) | async-done | bytes 8388624 | tf_op jit(solution)/shard_map/psum | solution.py:57
  249.1 0.0 all-reduce.5.cloned.1.call-update
  249.1 0.8 copy.17
  249.8 173.5 %all-reduce.5.cloned.1.call-done = (f32[1024,1024]{1,0:T(8,128)}, f32[1024,1024]{1,0:T(8,128)}) async-done(((f32[1024,1024]{1,0:T(8,128)}, f32[1024,1024]{1,0:T(8,128)}), (f32[1024,1024]{1,0:T(8,128)}, f32[1024,1024]{1,0:T(8,128)})) %all-reduce.5.cloned.1.call-update) | async-done | bytes 8388624 | tf_op jit(solution)/shard_map/psum | solution.py:57
  423.3 8.9 %broadcast_multiply_fusion = (f32[1024,1024]{1,0:T(8,128)}, f32[1024,1024]{1,0:T(8,128)}) fusion(f32[1024,1024]{1,0:T(8,128)} %get-tuple-element.13, f32[1024,1024]{1,0:T(8,128)} %get-tuple-element.12), kind=kLoop, calls=%fused_computation.2 | loop fusion | flops 2097152 | bytes 16777216 | tf_op jit(solution)/shard_map/mul | solution.py:59
  (4 shorter events, 0.0 us)
Async XLA Ops:
  10.4 30.3 %all-to-all-start = ((bf16[2,2,1024,128]{3,1,0,2:T(2,128)(2,1)}), bf16[2,2,1024,128]{3,1,0,2:T(2,128)(2,1)S(1)}, u32[]{:S(2)}, u32[]{:S(2)}) async-start(bf16[2,2,1024,128]{3,1,0,2:T(2,128)(2,1)} %copy.14), calls=%async_computation | async-start | bytes 2097152 | tf_op jit(solution)/shard_map/all_to_all | solution.py:52
  17.8 231.2 %all-reduce.7.cloned.1.call-start = ((), (), s32[]{:S(2)}) async-start(), calls=%async_computation.2 | async-start | bytes 16777216 | tf_op jit(solution)/shard_map/psum | solution.py:57
  48.7 374.6 %all-reduce.5.cloned.1.call-start = ((), (), s32[]{:S(2)}) async-start(), calls=%async_computation.1 | async-start | bytes 16777216 | tf_op jit(solution)/shard_map/psum | solution.py:57
Sparse Core Ops, SparseCore 0:
  48.8 200.2 all-reduce.6
  252.8 170.4 all-reduce.4
